TPU v7x, 32 devices: a whole 2x2x4 slice. The times are simulated.
32 devices in a mesh: grp: 2 (over y), seq: 4 (over z), head: 2 (over x), rep: 2 (over core).
Axes of the slice: x: 2, y: 2, z: 4, core: 2. Of those that a mesh axis runs over, the one named last changes fastest.
Arguments:
- queries: bfloat16 [16, 4096], P(('grp', 'rep'), 'head'), parts along dimension 0, may hold values from -6 to 6
- k_cache: bfloat16 [16, 16, 4096, 128], P(('grp', 'rep'), 'head', 'seq'), parts along dimension 0, may hold values from -6 to 6
- v_cache: bfloat16 [16, 16, 4096, 128], P(('grp', 'rep'), 'head', 'seq'), parts along dimension 0, may hold values from -6 to 6
- page_table: int32 [16, 32], P(('grp', 'rep')), parts along dimension 0, may hold values from 0 to 31, each once within a row
- lengths: int32 [16], P(('grp', 'rep')), parts along dimension 0, may hold values from 512 to 4096
- keep_threshold: int32 [16, 16], P(('grp', 'rep'), 'head'), parts along dimension 0, may hold values from 256 to 8191
Outputs:
- attended: bfloat16 [16, 4096], P(('grp', 'rep'), 'head'), parts along dimension 0
- token_mass: float32 [16, 16, 4096], P(('grp', 'rep'), 'head', 'seq'), parts along dimension 0
- page_keep: float32 [16, 16, 32], P(('grp', 'rep'), 'head', 'seq'), parts along dimension 0
There are 2 independent parts, one for each index of `grp`. A program takes and returns all parts, laid end to end along the dimension named above; each array names one. Nothing has to cross between parts.
Inputs may be any that keep to these rules, and one draw needn't show every extreme that they name: `page_table`: each row names every physical page slot 0 to 31 once.
All inputs are finite; a program needn't handle non-finite values.
Results may differ from a plain program's by a relative error of at most 0.0052.
Values sent between devices are 32-bit elements; how exact they have to be, the bound alone decides.
A program may use at most 64 MiB of HBM per device.

v0:
```python
import jax
import jax.numpy as jnp
from jax import lax
from jax.sharding import PartitionSpec as P

PAGE = 128


softcap = 50.0
query_scale = 1.0 / 12.0
quanta = 65536.0


def shards(queries, k_cache, v_cache, page_table, lengths, keep_threshold):
    requests, kv_local, tok_local, head_size = k_cache.shape
    q_local = queries.shape[1] // head_size
    group = q_local // kv_local
    pages_local = tok_local // PAGE
    pages_all = page_table.shape[1]
    seq_index = lax.axis_index("seq")
    slot_ids = seq_index * pages_local + jnp.arange(pages_local, dtype=jnp.int32)
    matches = page_table[:, None, :] == slot_ids[None, :, None]
    logical = jnp.sum(
        jnp.where(matches, jnp.arange(pages_all, dtype=jnp.int32)[None, None, :], 0), axis=2
    )
    position = (
        logical[:, :, None] * PAGE + jnp.arange(PAGE, dtype=jnp.int32)[None, None, :]
    ).reshape(requests, tok_local)
    is_live = position < lengths[:, None]
    grouped = queries.reshape(requests, kv_local, group, head_size)
    logits = jnp.einsum("rkgd,rktd->rkgt", grouped, k_cache, preferred_element_type=jnp.float32)
    capped = softcap * jnp.tanh(logits * query_scale / softcap)
    weights = jnp.where(is_live[:, None, None, :], jnp.exp(capped - softcap), 0.0)
    denom_part = jnp.sum(weights, axis=3)
    numer_part = jnp.einsum(
        "rkgt,rktd->rkgd", weights.astype(jnp.bfloat16), v_cache, preferred_element_type=jnp.float32
    )
    denom, numer = lax.psum((denom_part, numer_part), "seq")
    attended = (
        (numer / denom[..., None]).astype(jnp.bfloat16).reshape(requests, q_local * head_size)
    )
    payload = jnp.sum(weights / denom[..., None], axis=2).reshape(
        requests, kv_local, pages_local, PAGE
    )
    mine = seq_index * pages_local + jnp.arange(pages_local, dtype=jnp.int32)
    my_pages = jnp.sum(
        jnp.where(
            jnp.arange(pages_all, dtype=jnp.int32)[None, None, :] == mine[None, :, None],
            page_table[:, None, :],
            0,
        ),
        axis=2,
    )
    piece = lax.all_gather(payload, "seq", axis=2, tiled=True)
    count = piece.shape[2]
    phys = jnp.arange(count, dtype=jnp.int32)
    select = (my_pages[:, None, :] == phys[None, :, None]).astype(jnp.float32)
    owned = jnp.einsum("rxic,rim->rxmc", piece, select, precision=lax.Precision.HIGHEST)
    owned = owned.reshape(requests, payload.shape[1], tok_local)
    page_mass = jnp.sum(owned.reshape(requests, kv_local, pages_local, PAGE), axis=3)
    page_keep = jnp.minimum(
        1.0, quanta * page_mass / keep_threshold.astype(jnp.float32)[:, :, None]
    )
    return (attended, owned, page_keep)


def solution(mesh):
    placed = (
        P(("grp", "rep"), "head"),
        P(("grp", "rep"), "head", "seq", None),
        P(("grp", "rep"), "head", "seq", None),
        P(("grp", "rep"), None),
        P(("grp", "rep")),
        P(("grp", "rep"), "head"),
    )
    return jax.shard_map(
        shards,
        mesh=mesh,
        in_specs=placed,
        out_specs=(
            P(("grp", "rep"), "head"),
            P(("grp", "rep"), "head", "seq"),
            P(("grp", "rep"), "head", "seq"),
        ),
        check_vma=False,
    )
```

profile of v0, /device:TPU:0, one launch (start us, length us, event | category | flops | bytes accessed | tf_op | source)
XLA Modules:
  0.0 49.7 jit_solution(6556114332655537389)
XLA Ops:
  0.6 0.1 iota_compare_fusion.1
  0.7 0.9 %select_reduce_fusion = (s32[4,8]{1,0:T(4,128)S(1)}, s32[4,8]{1,0:T(4,128)S(1)}) fusion(s32[4,32]{1,0:T(4,128)} %param.9, pred[8,32]{1,0:T(8,128)(4,1)S(1)} %iota_compare_fusion.1, s32[8]{0:T(128)S(1)} %iota_add_fusion), kind=kLoop, calls=%fused_computation.16 | loop fusion | flops 5056 | bytes 1056 | tf_op jit(solution)/shard_map/reduce_sum | solution.py:46
  1.6 0.1 broadcast_bitcast_fusion
  1.7 0.7 %fusion.7 = pred[4,1024]{1,0:T(4,128)(4,1)S(1)} fusion(s32[1,4,8,128]{3,2,1,0:T(8,128)S(1)} %broadcast_bitcast_fusion, s32[4]{0:T(128)} %param.10, s32[1024]{0:T(1024)S(1)} %iota_bitcast_fusion), kind=kLoop, calls=%fused_computation.13 | loop fusion | flops 8192 | bytes 24592 | tf_op jit(solution)/shard_map/lt | solution.py:29
  2.5 0.7 %reshape.75 = bf16[4,8,2,128]{3,2,1,0:T(2,128)(2,1)S(1)} reshape(bf16[4,2048]{1,0:T(4,128)(2,1)} %param.6) | data formatting | bytes 32768 | tf_op jit(solution)/shard_map/reshape | solution.py:30
  3.2 0.0 copy-start
  3.2 0.0 copy-start.1
  3.2 5.9 %fusion.11 = (f32[4,8,2]{2,1,0:T(8,128)S(1)}, f32[4,8,2,1024]{3,2,1,0:T(2,128)S(1)}) fusion(bf16[4,8,2,128]{3,2,1,0:T(2,128)(2,1)S(1)} %reshape.75, bf16[4,8,1024,128]{3,2,1,0:T(8,128)(2,1)} %param.7, pred[4,1024]{1,0:T(4,128)(4,1)S(1)} %fusion.7), kind=kOutput, calls=%fused_computation.25 | convolution fusion | flops 17104832 | bytes 8671488 | tf_op jit(solution)/shard_map/rkgd,rktd->rkgt/dot_general | solution.py:31
  9.1 0.0 copy-done
  9.1 1.2 %fusion.5 = f32[4,8,2,128]{3,2,1,0:T(2,128)S(1)} fusion(bf16[4,8,1024,128]{3,2,1,0:T(8,128)(2,1)S(1)} %copy-done, f32[4,8,2,1024]{3,2,1,0:T(2,128)S(1)} %get-tuple-element.8), kind=kOutput, calls=%fused_computation.9 | convolution fusion | flops 16842752 | bytes 8683520 | tf_op jit(solution)/shard_map/rkgt,rktd->rkgd/dot_general | solution.py:35
  10.3 21.4 %all-reduce = (f32[4,8,2,128]{3,2,1,0:T(2,128)S(1)}, f32[4,8,2]{2,1,0:T(8,128)S(1)}) all-reduce(f32[4,8,2,128]{3,2,1,0:T(2,128)S(1)} %fusion.5, f32[4,8,2]{2,1,0:T(8,128)S(1)} %get-tuple-element.7), channel_id=1, replica_groups=mesh['grp'=2,'seq'=4,'head'=2,'rep'=2] {'seq'}, use_global_device_ids=true, to_apply=%region_1.2 | all-reduce | flops 8256 | bytes 66048 | tf_op jit(solution)/shard_map/psum | solution.py:38
  31.8 0.1 divide_convert_fusion
  31.9 0.6 %reshape.76 = bf16[4,2048]{1,0:T(4,128)(2,1)} reshape(bf16[4,8,2,128]{3,2,1,0:T(2,128)(2,1)S(1)} %divide_convert_fusion) | data formatting | bytes 32768 | tf_op jit(solution)/shard_map/reshape | solution.py:40
  32.5 0.4 divide_reduce_fusion
  32.9 15.0 %all_gather.3 = f32[4,8,32,128]{3,2,1,0:T(8,128)S(1)} all-gather(f32[4,8,8,128]{3,2,1,0:T(8,128)S(1)} %copy.14), channel_id=1, replica_groups=mesh['grp'=2,'seq'=4,'head'=2,'rep'=2] {'seq'}, dimensions={2}, use_global_device_ids=true | all-gather | bytes 655360 | tf_op jit(solution)/shard_map/all_gather | solution.py:54
  48.0 0.4 fusion.12
  48.4 0.7 %reshape.78 = f32[4,8,1024]{2,1,0:T(8,128)} reshape(f32[4,8,8,128]{3,2,1,0:T(8,128)S(1)} %get-tuple-element.10) | data formatting | bytes 262144 | tf_op jit(solution)/shard_map/reshape | solution.py:59
  49.1 0.0 copy-done.1
  49.1 0.7 %divide_minimum_fusion = f32[4,8,8]{2,1,0:T(8,128)} fusion(f32[4,8,8]{2,1,0:T(8,128)S(1)} %get-tuple-element.9, f32[4,8]{1,0:T(4,128)S(1)} %convert_element_type.12), kind=kLoop, calls=%fused_computation.14 | loop fusion | flops 768 | bytes 2176 | tf_op jit(solution)/shard_map/min | solution.py:61
  (5 shorter events, 0.0 us)
Async XLA Ops:
  3.2 5.9 %copy-start = (bf16[4,8,1024,128]{3,2,1,0:T(8,128)(2,1)S(1)}, bf16[4,8,1024,128]{3,2,1,0:T(8,128)(2,1)}, u32[]{:S(2)}) copy-start(bf16[4,8,1024,128]{3,2,1,0:T(8,128)(2,1)} %param.8) | copy-start | bytes 25165828
  3.2 45.9 %copy-start.1 = (s32[4,8]{1,0:T(4,128)S(1)}, s32[4,8]{1,0:T(4,128)}, u32[]{:S(2)}) copy-start(s32[4,8]{1,0:T(4,128)} %param.11) | copy-start | bytes 388
where the time goes:
time: 50 us; the launch traced here: 49.7 us
  blocking collectives  36.5 us (73%)
  matrix products  7.5 us (15%)
  other arithmetic  2.94 us (6%)
  local copies, waits for them, and re-layouts  2.15 us (4%)
  between operations  0.71 us (1%)
    psum x1, blocking collectives, shards(): denom, numer = lax.psum((denom_part, numer_part), 'seq')  21.4 us
    all_gather x1, blocking collectives, shards(): piece = lax.all_gather(payload, 'seq', axis=2, tiled=True)  15 us
    dot_general x1, matrix products, shards(): jnp.einsum('rkgd,rktd->rkgt', grouped, k_cache, preferred_element_type=jn...  5.9 us
    dot_general x1, matrix products, shards(): jnp.einsum('rkgt,rktd->rkgd', weights.astype(jnp.bfloat16), v_cache, pref...  1.23 us

commit v1 on v0

v1 whole, which is shorter than its diff:
```python
import functools

import jax
import jax.numpy as jnp
from jax import lax
from jax.experimental import pallas as pl
from jax.experimental.pallas import tpu as pltpu
from jax.sharding import PartitionSpec as P

PAGE = 128

softcap = 50.0
query_scale = 1.0 / 12.0
quanta = 65536.0
MESH = pl.DeviceIdType.MESH


def kernel(n, R, KV, G, T, D, *refs):
    (pt_s, len_s, pt_v, q_ref, k_hbm, v_hbm, tm_ref, pm_ref, at_ref) = refs[:9]
    kbuf, vbuf, qbd, maskb, wbuf, dn, nb = refs[9:16]
    gat = refs[16 : 16 + R]
    com = refs[16 + R : 16 + 2 * R]
    ksem, vsem, ds, dr, gs, gr, cs, cr, ns, nr = refs[16 + 2 * R :]
    HG = KV * G
    PL = T // PAGE
    TT = 2 * PAGE
    f32 = jnp.float32
    me = lax.axis_index("seq")

    def k_copy(r):
        return pltpu.make_async_copy(k_hbm.at[r], kbuf.at[r], ksem.at[r])

    def v_copy(r):
        return pltpu.make_async_copy(v_hbm.at[r], vbuf.at[r], vsem.at[r])

    for r in range(R):
        k_copy(r).start()
    for r in range(R):
        v_copy(r).start()

    barrier = pltpu.get_barrier_semaphore()
    for o in range(1, n):
        pl.semaphore_signal(
            barrier, inc=1, device_id={"seq": lax.rem(me + o, n)}, device_id_type=MESH
        )

    row16 = lax.broadcasted_iota(jnp.int32, (HG, 128), 0)
    lane16 = lax.broadcasted_iota(jnp.int32, (HG, 128), 1)
    rowk = lax.rem(row16, KV)

    for r in range(R):
        rows = jnp.concatenate(
            [
                q_ref[r : r + 1, (k * G + g) * D : (k * G + g + 1) * D].astype(f32)
                for g in range(G)
                for k in range(KV)
            ],
            axis=0,
        )
        for k in range(KV):
            qbd[r, :, k * D : (k + 1) * D] = jnp.where(rowk == k, rows, 0.0).astype(jnp.bfloat16)
    pages = pt_v.shape[1]
    slot = me * PL + lax.broadcasted_iota(jnp.int32, (PL, pages), 0)
    jpos = lax.broadcasted_iota(jnp.int32, (PL, pages), 1).astype(f32)
    tok = lax.broadcasted_iota(jnp.int32, (PL, PAGE), 1).astype(f32)
    for r in range(R):
        logical = jnp.sum(
            jnp.where(pt_v[r : r + 1, :] == slot, jpos, 0.0), axis=1, keepdims=True
        )
        limit = len_s[r].astype(f32) - logical * float(PAGE)
        maskb[r] = jnp.where(tok < limit, 1.0, 0.0)

    pl.semaphore_wait(barrier, n - 1)

    def d_copy(r, o):
        return pltpu.make_async_remote_copy(
            src_ref=dn.at[me, r],
            dst_ref=dn.at[me, r],
            send_sem=ds.at[r, o - 1],
            recv_sem=dr.at[r, o - 1],
            device_id={"seq": lax.rem(me + o, n)},
            device_id_type=MESH,
        )

    def scores(r, carry):
        k_copy(r).wait()
        mk = maskb[r]
        total = jnp.zeros((HG, PAGE), f32)
        for t in range(T // TT):
            acc = jnp.zeros((HG, TT), f32)
            for p in range(0, KV, 2):
                kp = jnp.concatenate(
                    [kbuf[r, p, t * TT : (t + 1) * TT, :], kbuf[r, p + 1, t * TT : (t + 1) * TT, :]],
                    axis=1,
                )
                acc += lax.dot_general(
                    qbd[r, :, p * D : (p + 2) * D],
                    kp,
                    (((1,), (1,)), ((), ())),
                    preferred_element_type=f32,
                )
            capped = softcap * jnp.tanh(acc * (query_scale / softcap))
            e = jnp.exp(capped - softcap)
            for c in range(TT // PAGE):
                m = mk[t * (TT // PAGE) + c : t * (TT // PAGE) + c + 1, :]
                w = jnp.where(m > 0.0, e[:, c * PAGE : (c + 1) * PAGE], 0.0)
                lo = t * TT + c * PAGE
                wbuf[r, :, lo : lo + PAGE] = w
                total += w
        col = jnp.sum(total, axis=1, keepdims=True)
        dn[me, r] = jnp.sum(jnp.where(row16 == lane16, col, 0.0), axis=0, keepdims=True)
        for o in range(1, n):
            d_copy(r, o).start()
        return carry

    lax.fori_loop(0, R, scores, 0)

    def denom_of(r):
        tot = dn[0, r]
        for s in range(1, n):
            tot = tot + dn[s, r]
        return jnp.sum(jnp.where(row16 == lane16, tot, 0.0), axis=1, keepdims=True)

    def is_mid(i):
        return jnp.logical_and(i > 0, i < n - 1)

    def g_copy(r, o):
        return pltpu.make_async_remote_copy(
            src_ref=gat[r].at[pl.ds(me * PL, PL)],
            dst_ref=gat[r].at[pl.ds(me * PL, PL)],
            send_sem=gs.at[r, o - 1],
            recv_sem=gr.at[r, o - 1],
            device_id={"seq": lax.rem(me + o, n)},
            device_id_type=MESH,
        )

    def c_copy(r, side):
        return pltpu.make_async_remote_copy(
            src_ref=com[r].at[side],
            dst_ref=gat[r].at[pl.ds(n * PL, PL)],
            send_sem=cs.at[r, side],
            recv_sem=cr.at[r],
            device_id={"seq": (n - 1) * side},
            device_id_type=MESH,
        )

    order = sorted(range(1, n), key=lambda o: -min(o, n - o))
    for r in range(R):
        for o in range(1, n):
            d_copy(r, o).wait_recv()
        den = denom_of(r)
        for c in range(PL):
            w = wbuf[r, :, c * PAGE : (c + 1) * PAGE] / den
            mass = w[0:KV]
            for g in range(1, G):
                mass = mass + w[g * KV : (g + 1) * KV]
            gat[r][me * PL + c] = mass
        for o in order:

            @pl.when(is_mid(lax.rem(me + o, n)))
            def _():
                g_copy(r, o).start()

    def n_copy(r, o):
        return pltpu.make_async_remote_copy(
            src_ref=nb.at[me, r],
            dst_ref=nb.at[me, r],
            send_sem=ns.at[r, o - 1],
            recv_sem=nr.at[r, o - 1],
            device_id={"seq": lax.rem(me + o, n)},
            device_id_type=MESH,
        )

    def mix(r, carry):
        v_copy(r).wait()
        out = jnp.zeros((HG, D), f32)
        for p in range(0, KV, 2):
            acc = jnp.zeros((HG, 2 * D), f32)
            for t in range(T // TT):
                vp = jnp.concatenate(
                    [vbuf[r, p, t * TT : (t + 1) * TT, :], vbuf[r, p + 1, t * TT : (t + 1) * TT, :]],
                    axis=1,
                )
                acc += jnp.dot(
                    wbuf[r, :, t * TT : (t + 1) * TT].astype(jnp.bfloat16),
                    vp,
                    preferred_element_type=f32,
                )
            out = jnp.where(rowk == p, acc[:, :D], out)
            out = jnp.where(rowk == p + 1, acc[:, D:], out)
        nb[me, r] = out
        for o in range(1, n):
            n_copy(r, o).start()
        return carry

    lax.fori_loop(0, R, mix, 0)

    for r in range(R):

        @pl.when(is_mid(me))
        def _():
            for o in range(1, n):
                g_copy(r, o).wait_recv()

        for side in (0, 1):

            @pl.when(me == (1 if side == 0 else n - 2))
            def _():
                for m in range(PL):
                    com[r][side, m] = gat[r][pt_s[r, side * (n - 1) * PL + m]]
                c_copy(r, side).start()

    lane_pl = lax.broadcasted_iota(jnp.int32, (KV, PAGE), 1)
    at_end = jnp.logical_not(is_mid(me))
    for r in range(R):

        @pl.when(at_end)
        def _():
            c_copy(r, 0).wait_recv()

        sums = jnp.zeros((KV, PAGE), f32)
        for m in range(PL):
            p = pt_s[r, me * PL + m]
            away = jnp.logical_or(p < me * PL, p >= (me + 1) * PL)
            idx = jnp.where(jnp.logical_and(at_end, away), n * PL + m, p)
            page = gat[r][idx]
            tm_ref[r, :, m * PAGE : (m + 1) * PAGE] = page
            sums = jnp.where(lane_pl == m, jnp.sum(page, axis=1, keepdims=True), sums)
        pm_ref[r] = sums[:, :PL]

    for r in range(R):
        for o in range(1, n):
            n_copy(r, o).wait_recv()
        tot = nb[0, r]
        for s in range(1, n):
            tot = tot + nb[s, r]
        at_ref[r] = tot / denom_of(r)

    for r in range(R):
        for o in range(1, n):
            d_copy(r, o).wait_send()
            n_copy(r, o).wait_send()

            @pl.when(is_mid(lax.rem(me + o, n)))
            def _():
                g_copy(r, o).wait_send()

        for side in (0, 1):

            @pl.when(me == (1 if side == 0 else n - 2))
            def _():
                c_copy(r, side).wait_send()


def shards(n, queries, k_cache, v_cache, page_table, lengths, keep_threshold):
    R, KV, T, D = k_cache.shape
    G = queries.shape[1] // D // KV
    HG = KV * G
    PL = T // PAGE
    f32 = jnp.float32
    vmem = pl.BlockSpec(memory_space=pltpu.VMEM)
    smem = pl.BlockSpec(memory_space=pltpu.SMEM)
    hbm = pl.BlockSpec(memory_space=pl.ANY)
    dma = pltpu.SemaphoreType.DMA
    owned, mass, att = pl.pallas_call(
        functools.partial(kernel, n, R, KV, G, T, D),
        out_shape=(
            jax.ShapeDtypeStruct((R, KV, T), f32),
            jax.ShapeDtypeStruct((R, KV, PL), f32),
            jax.ShapeDtypeStruct((R, HG, D), f32),
        ),
        in_specs=[smem, smem, vmem, vmem, hbm, hbm],
        out_specs=(vmem, vmem, vmem),
        scratch_shapes=[
            pltpu.VMEM((R, KV, T, D), jnp.bfloat16),
            pltpu.VMEM((R, KV, T, D), jnp.bfloat16),
            pltpu.VMEM((R, HG, KV * D), jnp.bfloat16),
            pltpu.VMEM((R, PL, PAGE), f32),
            pltpu.VMEM((R, HG, T), f32),
            pltpu.VMEM((n, R, 1, 128), f32),
            pltpu.VMEM((n, R, HG, D), f32),
        ]
        + [pltpu.VMEM(((n + 1) * PL, KV, PAGE), f32)] * R
        + [pltpu.VMEM((2, PL, KV, PAGE), f32)] * R
        + [
            dma((R,)),
            dma((R,)),
            dma((R, n - 1)),
            dma((R, n - 1)),
            dma((R, n - 1)),
            dma((R, n - 1)),
            dma((R, 2)),
            dma((R,)),
            dma((R, n - 1)),
            dma((R, n - 1)),
        ],
        compiler_params=pltpu.CompilerParams(collective_id=0, has_side_effects=True),
    )(page_table, lengths, page_table, queries, k_cache, v_cache)
    attended = (
        att.reshape(R, G, KV, D).transpose(0, 2, 1, 3).reshape(R, HG * D).astype(jnp.bfloat16)
    )
    page_keep = jnp.minimum(1.0, quanta * mass / keep_threshold.astype(f32)[:, :, None])
    return attended, owned, page_keep


def solution(mesh):
    placed = (
        P(("grp", "rep"), "head"),
        P(("grp", "rep"), "head", "seq", None),
        P(("grp", "rep"), "head", "seq", None),
        P(("grp", "rep"), None),
        P(("grp", "rep")),
        P(("grp", "rep"), "head"),
    )
    return jax.shard_map(
        functools.partial(shards, mesh.shape["seq"]),
        mesh=mesh,
        in_specs=placed,
        out_specs=(
            P(("grp", "rep"), "head"),
            P(("grp", "rep"), "head", "seq"),
            P(("grp", "rep"), "head", "seq"),
        ),
        check_vma=False,
    )
```

time: 50 us -> 29.3 us (0.59)
  blocking collectives: 36.5 us -> 0 us
  Pallas kernels: 0 us -> 23.2 us
  matrix products: 7.5 us -> 0 us
    pallas_call x0 -> x1, Pallas kernels: none -> 23.2 us  [shards(): pl.pallas_call(functools.partial(kernel, n, R, KV, G, T, D), out_shape=(j...]
    psum x1 -> x0, blocking collectives: 21.4 us -> none  [shards(): denom, numer = lax.psum((denom_part, numer_part), 'seq')]
    all_gather x1 -> x0, blocking collectives: 15 us -> none  [shards(): piece = lax.all_gather(payload, 'seq', axis=2, tiled=True)]
    dot_general x3 -> x0, matrix products: 7.5 us -> none  [the longest x1 5.9 us: shards(): jnp.einsum('rkgd,rktd->rkgt', grouped, k_cache, preferred_element_type=jn...]
    reshape x3 -> x0, local copies, waits for them, and re-layouts: 2.03 us -> none  [the longest x1 0.73 us: shards(): grouped = queries.reshape(requests, kv_local, group, head_size)]
    unnamed x6 -> x1, local copies, waits for them, and re-layouts: 0.11 us -> 1.57 us
    convert_element_type x2, other arithmetic: 0.11 us -> 1.45 us  [the longest x1 0.76 us: shards(): att.reshape(R, G, KV, D).transpose(0, 2, 1, 3).reshape(R, HG * D)]
    reduce_sum x2 -> x0, other arithmetic: 1.32 us -> none  [the longest x1 0.91 us: shards(): jnp.sum(jnp.where(jnp.arange(pages_all, dtype=jnp.int32)[None, None, :] =...]
where the time goes in v1:
time: 29.3 us; the launch traced here: 28.9 us
  Pallas kernels  23.2 us (79%)
  other arithmetic  2.85 us (10%)
  local copies, waits for them, and re-layouts  2.2 us (8%)
  between operations  0.64 us (2%)
    pallas_call x1, Pallas kernels, shards(): pl.pallas_call(functools.partial(kernel, n, R, KV, G, T, D), out_shape=(j...  23.2 us
    unnamed x1, local copies, waits for them, and re-layouts  1.57 us
    min x1, other arithmetic, shards(): jnp.minimum(1.0, quanta * mass / keep_threshold.astype(f32)[:, :, None])  1.4 us
    convert_element_type x1, other arithmetic, shards(): att.reshape(R, G, KV, D).transpose(0, 2, 1, 3).reshape(R, HG * D)  0.76 us
    convert_element_type x1, other arithmetic, shards(): keep_threshold.astype(f32)[:, :, None]  0.68 us
    convert_element_type x2, local copies, waits for them, and re-layouts, shards(): att.reshape(R, G, KV, D).transpose(0, 2, 1, 3).reshape(R, HG * D)  0.63 us

profile of v1, /device:TPU:0, one launch (start us, length us, event | category | flops | bytes accessed | tf_op | source)
XLA Modules:
  0.0 28.9 jit_solution(7807815059551757328)
XLA Ops:
  0.6 0.7 %convert_element_type.19 = f32[4,8]{1,0:T(4,128)S(1)} convert(s32[4,8]{1,0:T(4,128)} %param.11) | non-fusion elementwise | flops 32 | bytes 256 | tf_op jit(solution)/shard_map/convert_element_type | solution.py:302
  1.3 23.2 %shard_map.85 = (f32[4,8,1024]{2,1,0:T(8,128)}, f32[4,8,8]{2,1,0:T(8,128)}, f32[4,16,128]{2,1,0:T(8,128)}) custom-call(s32[4,32]{1,0:T(4,128)} %refs_2_.1, s32[4]{0:T(128)} %refs_1_.1, s32[4,32]{1,0:T(4,128)} %refs_2_.1, bf16[4,2048]{1,0:T(4,128)(2,1)} %refs_3_.1, bf16[4,8,1024,128]{3,2,1,0:T(8,128)(2,1)} %refs_4_.1, bf16[4,8,1024,128]{3,2,1,0:T(8,128)(2,1)} %refs_5_.1), custom_call_target="tpu_custom_call" | custom-call | tf_op jit(solution)/shard_map/pallas_call | solution.py:265
  24.5 0.8 %convert_bitcast_fusion = bf16[4,8,2,128]{3,1,2,0:T(8,128)(2,1)S(1)} fusion(f32[4,16,128]{2,1,0:T(8,128)} %get-tuple-element.6), kind=kLoop, calls=%fused_computation.1 | loop fusion | flops 8192 | bytes 49152 | tf_op jit(solution)/shard_map/convert_element_type | solution.py:300
  25.3 0.6 %convert_element_type.18 = bf16[4,2048]{1,0:T(4,128)(2,1)} reshape(bf16[4,8,2,128]{3,2,1,0:T(2,128)(2,1)S(1)} %copy.9) | data formatting | bytes 32768 | tf_op jit(solution)/shard_map/convert_element_type | solution.py:300
  25.9 1.4 %divide_minimum_fusion = f32[4,8,8]{2,1,0:T(8,128)} fusion(f32[4,8,8]{2,1,0:T(8,128)} %get-tuple-element.8, f32[4,8]{1,0:T(4,128)S(1)} %convert_element_type.19), kind=kLoop, calls=%fused_computation | loop fusion | flops 768 | bytes 2176 | tf_op jit(solution)/shard_map/min | solution.py:302
  27.3 1.6 %copy.11 = f32[4,8,1024]{2,1,0:T(8,128)} copy(f32[4,8,1024]{2,1,0:T(8,128)} %get-tuple-element.13) | data formatting | bytes 262144
  (1 shorter events, 0.0 us)

commit v2 on v1

--- a/solution.py
+++ b/solution.py
@@ -16,11 +16,11 @@
 
 
 def kernel(n, R, KV, G, T, D, *refs):
-    (pt_s, len_s, pt_v, q_ref, k_hbm, v_hbm, tm_ref, pm_ref, at_ref) = refs[:9]
-    kbuf, vbuf, qbd, maskb, wbuf, dn, nb = refs[9:16]
-    gat = refs[16 : 16 + R]
-    com = refs[16 + R : 16 + 2 * R]
-    ksem, vsem, ds, dr, gs, gr, cs, cr, ns, nr = refs[16 + 2 * R :]
+    (pt_s, len_s, pt_v, q_ref, k_hbm, v_hbm, tm_ref, at_ref) = refs[:8]
+    kbuf, vbuf, qbd, maskb, wbuf, dn, nb = refs[8:15]
+    gat = refs[15 : 15 + R]
+    com = refs[15 + R : 15 + 2 * R]
+    ksem, vsem, ds, dr, gs, gr, cs, cr, ns, nr = refs[15 + 2 * R :]
     HG = KV * G
     PL = T // PAGE
     TT = 2 * PAGE
@@ -35,9 +35,6 @@
 
     for r in range(R):
         k_copy(r).start()
-    for r in range(R):
-        v_copy(r).start()
-
     barrier = pltpu.get_barrier_semaphore()
     for o in range(1, n):
         pl.semaphore_signal(
@@ -84,6 +81,7 @@
 
     def scores(r, carry):
         k_copy(r).wait()
+        v_copy(r).start()
         mk = maskb[r]
         total = jnp.zeros((HG, PAGE), f32)
         for t in range(T // TT):
@@ -144,23 +142,6 @@
             device_id_type=MESH,
         )
 
-    order = sorted(range(1, n), key=lambda o: -min(o, n - o))
-    for r in range(R):
-        for o in range(1, n):
-            d_copy(r, o).wait_recv()
-        den = denom_of(r)
-        for c in range(PL):
-            w = wbuf[r, :, c * PAGE : (c + 1) * PAGE] / den
-            mass = w[0:KV]
-            for g in range(1, G):
-                mass = mass + w[g * KV : (g + 1) * KV]
-            gat[r][me * PL + c] = mass
-        for o in order:
-
-            @pl.when(is_mid(lax.rem(me + o, n)))
-            def _():
-                g_copy(r, o).start()
-
     def n_copy(r, o):
         return pltpu.make_async_remote_copy(
             src_ref=nb.at[me, r],
@@ -193,7 +174,26 @@
             n_copy(r, o).start()
         return carry
 
-    lax.fori_loop(0, R, mix, 0)
+    order = sorted(range(1, n), key=lambda o: -min(o, n - o))
+    def spread(r):
+        for o in range(1, n):
+            d_copy(r, o).wait_recv()
+        den = denom_of(r)
+        for c in range(PL):
+            w = wbuf[r, :, c * PAGE : (c + 1) * PAGE] / den
+            mass = w[0:KV]
+            for g in range(1, G):
+                mass = mass + w[g * KV : (g + 1) * KV]
+            gat[r][me * PL + c] = mass
+        for o in order:
+
+            @pl.when(is_mid(lax.rem(me + o, n)))
+            def _():
+                g_copy(r, o).start()
+
+    for r in range(R):
+        spread(r)
+        lax.fori_loop(r, r + 1, mix, 0)
 
     for r in range(R):
 
@@ -210,7 +210,6 @@
                     com[r][side, m] = gat[r][pt_s[r, side * (n - 1) * PL + m]]
                 c_copy(r, side).start()
 
-    lane_pl = lax.broadcasted_iota(jnp.int32, (KV, PAGE), 1)
     at_end = jnp.logical_not(is_mid(me))
     for r in range(R):
 
@@ -218,15 +217,12 @@
         def _():
             c_copy(r, 0).wait_recv()
 
-        sums = jnp.zeros((KV, PAGE), f32)
         for m in range(PL):
             p = pt_s[r, me * PL + m]
             away = jnp.logical_or(p < me * PL, p >= (me + 1) * PL)
             idx = jnp.where(jnp.logical_and(at_end, away), n * PL + m, p)
             page = gat[r][idx]
             tm_ref[r, :, m * PAGE : (m + 1) * PAGE] = page
-            sums = jnp.where(lane_pl == m, jnp.sum(page, axis=1, keepdims=True), sums)
-        pm_ref[r] = sums[:, :PL]
 
     for r in range(R):
         for o in range(1, n):
@@ -250,6 +246,30 @@
             @pl.when(me == (1 if side == 0 else n - 2))
             def _():
                 c_copy(r, side).wait_send()
+
+
+def finish(R, KV, G, T, D, own_ref, att_ref, keep_ref, at_ref, tm_ref, pk_ref, sem):
+    PL = T // PAGE
+    f32 = jnp.float32
+    out = pltpu.make_async_copy(own_ref, tm_ref, sem)
+    out.start()
+    for k in range(KV):
+        for g in range(G):
+            h = k * G + g
+            at_ref[:, h * D : (h + 1) * D] = att_ref[:, g * KV + k, :].astype(jnp.bfloat16)
+    lane = lax.broadcasted_iota(jnp.int32, (KV, PAGE), 1)
+    diag = lax.broadcasted_iota(jnp.int32, (KV, KV), 0) == lax.broadcasted_iota(
+        jnp.int32, (KV, KV), 1
+    )
+    for r in range(R):
+        sums = jnp.zeros((KV, PAGE), f32)
+        for m in range(PL):
+            page = own_ref[r, :, m * PAGE : (m + 1) * PAGE]
+            sums = jnp.where(lane == m, jnp.sum(page, axis=1, keepdims=True), sums)
+        row = keep_ref[r : r + 1, :].astype(f32)
+        keep = jnp.sum(jnp.where(diag, row, 0.0), axis=1, keepdims=True)
+        pk_ref[r] = jnp.minimum(1.0, quanta * sums / keep)[:, :PL]
+    out.wait()
 
 
 def shards(n, queries, k_cache, v_cache, page_table, lengths, keep_threshold):
@@ -262,15 +282,14 @@
     smem = pl.BlockSpec(memory_space=pltpu.SMEM)
     hbm = pl.BlockSpec(memory_space=pl.ANY)
     dma = pltpu.SemaphoreType.DMA
-    owned, mass, att = pl.pallas_call(
+    owned, att = pl.pallas_call(
         functools.partial(kernel, n, R, KV, G, T, D),
         out_shape=(
-            jax.ShapeDtypeStruct((R, KV, T), f32),
-            jax.ShapeDtypeStruct((R, KV, PL), f32),
-            jax.ShapeDtypeStruct((R, HG, D), f32),
+            pltpu.VMEM((R, KV, T), f32),
+            pltpu.VMEM((R, HG, D), f32),
         ),
         in_specs=[smem, smem, vmem, vmem, hbm, hbm],
-        out_specs=(vmem, vmem, vmem),
+        out_specs=(vmem, vmem),
         scratch_shapes=[
             pltpu.VMEM((R, KV, T, D), jnp.bfloat16),
             pltpu.VMEM((R, KV, T, D), jnp.bfloat16),
@@ -296,11 +315,19 @@
         ],
         compiler_params=pltpu.CompilerParams(collective_id=0, has_side_effects=True),
     )(page_table, lengths, page_table, queries, k_cache, v_cache)
-    attended = (
-        att.reshape(R, G, KV, D).transpose(0, 2, 1, 3).reshape(R, HG * D).astype(jnp.bfloat16)
-    )
-    page_keep = jnp.minimum(1.0, quanta * mass / keep_threshold.astype(f32)[:, :, None])
-    return attended, owned, page_keep
+    owned = pltpu.with_memory_space_constraint(owned, pltpu.VMEM)
+    att = pltpu.with_memory_space_constraint(att, pltpu.VMEM)
+    return pl.pallas_call(
+        functools.partial(finish, R, KV, G, T, D),
+        out_shape=(
+            jax.ShapeDtypeStruct((R, HG * D), jnp.bfloat16),
+            jax.ShapeDtypeStruct((R, KV, T), f32),
+            jax.ShapeDtypeStruct((R, KV, PL), f32),
+        ),
+        in_specs=[vmem, vmem, vmem],
+        out_specs=(vmem, hbm, vmem),
+        scratch_shapes=[dma],
+    )(owned, att, keep_threshold)
 
 
 def solution(mesh):

time: 29.3 us -> 25.7 us (0.88)
  other arithmetic: 2.85 us -> 0 us
  local copies, waits for them, and re-layouts: 2.2 us -> 0 us
  Pallas kernels: 23.2 us -> 24.7 us
    unnamed x1 -> x0, local copies, waits for them, and re-layouts: 1.57 us -> none
    pallas_call x1 -> x2, Pallas kernels: 23.2 us -> 24.7 us  [the longest x1 22.8 us: shards(): pl.pallas_call(functools.partial(kernel, n, R, KV, G, T, D), out_shape=(p...]
    convert_element_type x2 -> x0, other arithmetic: 1.45 us -> none  [the longest x1 0.76 us: shards(): att.reshape(R, G, KV, D).transpose(0, 2, 1, 3).reshape(R, HG * D)]
    min x1 -> x0, other arithmetic: 1.4 us -> none  [shards(): jnp.minimum(1.0, quanta * mass / keep_threshold.astype(f32)[:, :, None])]
    convert_element_type x2 -> x0, local copies, waits for them, and re-layouts: 0.63 us -> none  [shards(): att.reshape(R, G, KV, D).transpose(0, 2, 1, 3).reshape(R, HG * D)]
where the time goes in v2:
time: 25.7 us; the launch traced here: 25.4 us
  Pallas kernels  24.7 us (96%)
  between operations  0.64 us (2%)
    pallas_call x1, Pallas kernels, shards(): pl.pallas_call(functools.partial(kernel, n, R, KV, G, T, D), out_shape=(p...  22.8 us
    pallas_call x1, Pallas kernels, shards(): pl.pallas_call(functools.partial(finish, R, KV, G, T, D), out_shape=(jax....  1.96 us

profile of v2, /device:TPU:0, one launch (start us, length us, event | category | flops | bytes accessed | tf_op | source)
XLA Modules:
  0.0 25.4 jit_solution(5361107214915250195)
XLA Ops:
  0.6 22.8 %shard_map.85 = (f32[4,8,1024]{2,1,0:T(8,128)S(1)}, f32[4,16,128]{2,1,0:T(8,128)S(1)}) custom-call(s32[4,32]{1,0:T(4,128)} %refs_2_.1, s32[4]{0:T(128)} %refs_1_.1, s32[4,32]{1,0:T(4,128)} %refs_2_.1, bf16[4,2048]{1,0:T(4,128)(2,1)} %refs_3_.1, bf16[4,8,1024,128]{3,2,1,0:T(8,128)(2,1)} %refs_4_.1, bf16[4,8,1024,128]{3,2,1,0:T(8,128)(2,1)} %refs_5_.1), custom_call_target="tpu_custom_call" | custom-call | tf_op jit(solution)/shard_map/pallas_call | solution.py:285
  23.4 2.0 %shard_map.86 = (bf16[4,2048]{1,0:T(4,128)(2,1)}, f32[4,8,1024]{2,1,0:T(8,128)}, f32[4,8,8]{2,1,0:T(8,128)}) custom-call(f32[4,8,1024]{2,1,0:T(8,128)S(1)} %get-tuple-element.5.own_ref, f32[4,16,128]{2,1,0:T(8,128)S(1)} %get-tuple-element.6.att_ref, s32[4,8]{1,0:T(4,128)} %keep_ref.1), custom_call_target="tpu_custom_call" | custom-call | tf_op jit(solution)/shard_map/pallas_call | solution.py:320

commit v3 on v2

--- a/solution.py
+++ b/solution.py
@@ -17,11 +17,13 @@
 
 def kernel(n, R, KV, G, T, D, *refs):
     (pt_s, len_s, pt_v, q_ref, k_hbm, v_hbm, tm_ref, at_ref) = refs[:8]
-    kbuf, vbuf, qbd, maskb, wbuf, dn, nb = refs[8:15]
-    gat = refs[15 : 15 + R]
-    com = refs[15 + R : 15 + 2 * R]
-    ksem, vsem, ds, dr, gs, gr, cs, cr, ns, nr = refs[15 + 2 * R :]
+    kbuf, vbuf, qbd, maskb, wbuf, dn, nb, rb, ab, denb = refs[8:18]
+    gat = refs[18 : 18 + R]
+    com = refs[18 + R : 18 + 2 * R]
+    ksem, vsem, ds, dr, gs, gr, cs, cr, ns, nr, fs, fr = refs[18 + 2 * R :]
     HG = KV * G
+    rows_of = R * HG // n
+    parts = HG // rows_of
     PL = T // PAGE
     TT = 2 * PAGE
     f32 = jnp.float32
@@ -142,12 +144,22 @@
             device_id_type=MESH,
         )
 
-    def n_copy(r, o):
+    def n_copy(p, source):
         return pltpu.make_async_remote_copy(
-            src_ref=nb.at[me, r],
-            dst_ref=nb.at[me, r],
-            send_sem=ns.at[r, o - 1],
-            recv_sem=nr.at[r, o - 1],
+            src_ref=nb.at[p],
+            dst_ref=rb.at[source],
+            send_sem=ns.at[p],
+            recv_sem=nr.at[source],
+            device_id={"seq": p},
+            device_id_type=MESH,
+        )
+
+    def f_copy(o):
+        return pltpu.make_async_remote_copy(
+            src_ref=ab.at[me],
+            dst_ref=ab.at[me],
+            send_sem=fs.at[o - 1],
+            recv_sem=fr.at[o - 1],
             device_id={"seq": lax.rem(me + o, n)},
             device_id_type=MESH,
         )
@@ -169,9 +181,15 @@
                 )
             out = jnp.where(rowk == p, acc[:, :D], out)
             out = jnp.where(rowk == p + 1, acc[:, D:], out)
-        nb[me, r] = out
-        for o in range(1, n):
-            n_copy(r, o).start()
+        for j in range(parts):
+            nb[r * parts + j] = out[j * rows_of : (j + 1) * rows_of]
+        for j in range(parts):
+            dest = r * parts + j
+
+            @pl.when(dest != me)
+            def _():
+                n_copy(dest, me).start()
+
         return carry
 
     order = sorted(range(1, n), key=lambda o: -min(o, n - o))
@@ -179,6 +197,9 @@
         for o in range(1, n):
             d_copy(r, o).wait_recv()
         den = denom_of(r)
+        wide = jnp.broadcast_to(den, (HG, D))
+        for j in range(parts):
+            denb[r * parts + j] = wide[j * rows_of : (j + 1) * rows_of]
         for c in range(PL):
             w = wbuf[r, :, c * PAGE : (c + 1) * PAGE] / den
             mass = w[0:KV]
@@ -193,9 +214,24 @@
 
     for r in range(R):
         spread(r)
-        lax.fori_loop(r, r + 1, mix, 0)
-
-    for r in range(R):
+    lax.fori_loop(0, R, mix, 0)
+
+    def combine():
+        rb[me] = nb[me]
+        for s in range(n):
+
+            @pl.when(me != s)
+            def _():
+                n_copy(me, s).wait_recv()
+
+        tot = rb[0]
+        for s in range(1, n):
+            tot = tot + rb[s]
+        ab[me] = tot / denb[me]
+        for o in range(1, n):
+            f_copy(o).start()
+
+    def compact(r):
 
         @pl.when(is_mid(me))
         def _():
@@ -209,6 +245,12 @@
                 for m in range(PL):
                     com[r][side, m] = gat[r][pt_s[r, side * (n - 1) * PL + m]]
                 c_copy(r, side).start()
+
+    for r in range(R // 2):
+        compact(r)
+    combine()
+    for r in range(R // 2, R):
+        compact(r)
 
     at_end = jnp.logical_not(is_mid(me))
     for r in range(R):
@@ -224,18 +266,23 @@
             page = gat[r][idx]
             tm_ref[r, :, m * PAGE : (m + 1) * PAGE] = page
 
-    for r in range(R):
-        for o in range(1, n):
-            n_copy(r, o).wait_recv()
-        tot = nb[0, r]
-        for s in range(1, n):
-            tot = tot + nb[s, r]
-        at_ref[r] = tot / denom_of(r)
-
+    for o in range(1, n):
+        f_copy(o).wait_recv()
+    for r in range(R):
+        for j in range(parts):
+            at_ref[r, j * rows_of : (j + 1) * rows_of] = ab[r * parts + j]
+
+    for p in range(n):
+
+        @pl.when(me != p)
+        def _():
+            n_copy(p, me).wait_send()
+
+    for o in range(1, n):
+        f_copy(o).wait_send()
     for r in range(R):
         for o in range(1, n):
             d_copy(r, o).wait_send()
-            n_copy(r, o).wait_send()
 
             @pl.when(is_mid(lax.rem(me + o, n)))
             def _():
@@ -297,7 +344,10 @@
             pltpu.VMEM((R, PL, PAGE), f32),
             pltpu.VMEM((R, HG, T), f32),
             pltpu.VMEM((n, R, 1, 128), f32),
-            pltpu.VMEM((n, R, HG, D), f32),
+            pltpu.VMEM((n, R * HG // n, D), f32),
+            pltpu.VMEM((n, R * HG // n, D), f32),
+            pltpu.VMEM((n, R * HG // n, D), f32),
+            pltpu.VMEM((n, R * HG // n, D), f32),
         ]
         + [pltpu.VMEM(((n + 1) * PL, KV, PAGE), f32)] * R
         + [pltpu.VMEM((2, PL, KV, PAGE), f32)] * R
@@ -310,8 +360,10 @@
             dma((R, n - 1)),
             dma((R, 2)),
             dma((R,)),
-            dma((R, n - 1)),
-            dma((R, n - 1)),
+            dma((n,)),
+            dma((n,)),
+            dma((n - 1,)),
+            dma((n - 1,)),
         ],
         compiler_params=pltpu.CompilerParams(collective_id=0, has_side_effects=True),
     )(page_table, lengths, page_table, queries, k_cache, v_cache)

time: 25.7 us -> 25.2 us (0.981)
  Pallas kernels: 24.7 us -> 24.2 us
    pallas_call x1, Pallas kernels: 22.8 us -> 22.3 us  [shards(): pl.pallas_call(functools.partial(kernel, n, R, KV, G, T, D), out_shape=(p...]
where the time goes in v3:
time: 25.2 us; the launch traced here: 24.9 us
  Pallas kernels  24.2 us (96%)
  between operations  0.64 us (3%)
    pallas_call x1, Pallas kernels, shards(): pl.pallas_call(functools.partial(kernel, n, R, KV, G, T, D), out_shape=(p...  22.3 us
    pallas_call x1, Pallas kernels, shards(): pl.pallas_call(functools.partial(finish, R, KV, G, T, D), out_shape=(jax....  1.96 us

profile of v3, /device:TPU:0, one launch (start us, length us, event | category | flops | bytes accessed | tf_op | source)
XLA Modules:
  0.0 24.9 jit_solution(267123289794376069)
XLA Ops:
  0.6 22.3 %shard_map.85 = (f32[4,8,1024]{2,1,0:T(8,128)S(1)}, f32[4,16,128]{2,1,0:T(8,128)S(1)}) custom-call(s32[4,32]{1,0:T(4,128)} %refs_2_.1, s32[4]{0:T(128)} %refs_1_.1, s32[4,32]{1,0:T(4,128)} %refs_2_.1, bf16[4,2048]{1,0:T(4,128)(2,1)} %refs_3_.1, bf16[4,8,1024,128]{3,2,1,0:T(8,128)(2,1)} %refs_4_.1, bf16[4,8,1024,128]{3,2,1,0:T(8,128)(2,1)} %refs_5_.1), custom_call_target="tpu_custom_call" | custom-call | tf_op jit(solution)/shard_map/pallas_call | solution.py:332
  22.9 2.0 %shard_map.86 = (bf16[4,2048]{1,0:T(4,128)(2,1)}, f32[4,8,1024]{2,1,0:T(8,128)}, f32[4,8,8]{2,1,0:T(8,128)}) custom-call(f32[4,8,1024]{2,1,0:T(8,128)S(1)} %get-tuple-element.5.own_ref, f32[4,16,128]{2,1,0:T(8,128)S(1)} %get-tuple-element.6.att_ref, s32[4,8]{1,0:T(4,128)} %keep_ref.1), custom_call_target="tpu_custom_call" | custom-call | tf_op jit(solution)/shard_map/pallas_call | solution.py:372
